TPU v7x, 32 devices: a whole 2x2x4 slice. The times are simulated.
32 devices in a mesh: groups: 2 (over y), parts: 8 (over z, core), sub: 2 (over x), pair: 1.
Axes of the slice: x: 2, y: 2, z: 4, core: 2. Of those that a mesh axis runs over, the one named last changes fastest.
Arguments:
- spectra: bfloat16 [256, 128, 128], P(('groups', 'parts', 'pair')), parts along dimension 0, may hold values from -6 to 6
- defocus: bfloat16 [256], P(('groups', 'parts', 'pair')), parts along dimension 0, may hold values from 0.5 to 2
- classes: int32 [256, 4], P(('groups', 'parts', 'pair')), parts along dimension 0, may hold values from 0 to 7, all different within a row
- poses: int32 [256, 4], P(('groups', 'parts', 'pair')), parts along dimension 0, may hold values from 0 to 31
- probs: bfloat16 [256, 4], P(('groups', 'parts', 'pair')), parts along dimension 0, may hold values from 0.049804688 to 1
- counts: int32 [16], P(('groups', 'parts', 'pair')), parts along dimension 0, may hold values from 1 to 16, as said below
- offsets: int32 [32], replicated, may hold values from 0 to 64
- row_kernel: bfloat16 [32, 256, 64], P(None, 'sub'), may hold values from -0.015625 to 0.046875
- col_kernel: bfloat16 [32, 128, 64], replicated, may hold values from -0.015625 to 0.046875
Outputs:
- averages: float32 [16, 256, 256], P('groups', ('sub', 'pair')), parts along dimension 0
There are 2 independent parts, one for each index of `groups`. A program takes and returns all parts, laid end to end along the dimension named above; an argument that names none is the same for every part. Nothing has to cross between parts.
Inputs may be any that keep to these rules, and one draw needn't show every extreme that they name: Only the first counts slots of a shard hold used particles; some shard uses all 16 slots. The 4 classes of a particle differ.
All inputs are finite; a program needn't handle non-finite values.
Results may differ from a plain program's by a relative error of at most 0.0038.
Values may be sent and summed in bfloat16 or wider, within the bound.
A program may use at most 64 MiB of HBM per device.

v0:
```python
import functools
import math

import jax
import jax.numpy as jnp
import numpy as np
from jax import lax
from jax.experimental import pallas as pl
from jax.experimental.pallas import tpu as pltpu
from jax.sharding import PartitionSpec as P

GRID = 512
BOX = 256
IROWS = 128
ICOLS = 64
LROWS = 256
LCOLS = 128
BAND = 64
ITERS = 4

blob_width = 1.5
avg_scale = 8.0
floor_value = 1.0

f32 = jnp.float32
bf16 = jnp.bfloat16


def split_np(table):
    high = np.asarray(table, np.float32).astype(jnp.bfloat16)
    low = (table - high.astype(np.float64)).astype(np.float32).astype(jnp.bfloat16)
    return np.stack([high, low])


def tables(group_size):
    index = np.arange(GRID)
    distance = np.minimum(index, GRID - index).astype(np.float64)
    blob = np.exp(-2.0 * (math.pi * blob_width * distance / GRID) ** 2)
    beta = (blob[None, :] * np.cos(2 * np.pi * ((index[:, None] * index[None, :]) % GRID) / GRID)).sum(1)
    beta = beta / GRID
    rows = np.arange(LROWS)
    freq = rows - LROWS // 2
    cols = np.arange(LCOLS)
    factor = np.where(cols == 0, 1.0, 2.0)
    row_same = beta[(freq[:, None] - freq[None, :]) % GRID]
    row_flip = beta[(freq[:, None] + freq[None, :]) % GRID]
    row_table = np.concatenate([row_same, row_flip], axis=1)
    col_same = 0.5 * factor[:, None] * beta[(cols[:, None] - cols[None, :]) % GRID]
    col_flip = 0.5 * factor[:, None] * beta[(cols[:, None] + cols[None, :]) % GRID]
    col_table = np.concatenate([col_same, col_flip], axis=1)
    crop = np.arange(BOX) - BOX // 2
    correction = np.sinc(crop / GRID) ** 2
    angles = 2 * np.pi * ((crop[:, None] * cols[None, :]) % GRID) / GRID
    cos_c = factor[None, :] * np.cos(angles) / correction[:, None]
    sin_c = factor[None, :] * np.sin(angles) / correction[:, None]
    first = np.concatenate([cos_c, -sin_c], axis=1).reshape(group_size, -1, 2 * LCOLS)
    second = np.concatenate([sin_c, cos_c], axis=1).reshape(group_size, -1, 2 * LCOLS)
    out_cols = np.concatenate([first, second], axis=1)
    angles = 2 * np.pi * ((freq[:, None] * crop[None, :]) % GRID) / GRID
    scaling = avg_scale / GRID / correction[None, :]
    out_rows = np.concatenate([np.cos(angles) * scaling, -np.sin(angles) * scaling], axis=0)
    out_cols = np.swapaxes(split_np(out_cols), 0, 1)
    return split_np(row_table), split_np(col_table), out_cols, split_np(out_rows)


def sine_turns(turns):
    turns = turns - jnp.round(turns)
    half = jnp.where(turns < 0, -0.5, 0.5)
    turns = jnp.where(jnp.abs(turns) > 0.25, half - turns, turns)
    x = turns * (2.0 * math.pi)
    square = x * x
    value = jnp.full_like(x, -1.0 / math.factorial(11))
    for order in (9, 7, 5, 3, 1):
        sign = 1.0 if order % 4 == 1 else -1.0
        value = value * square + sign / math.factorial(order)
    return value * x


def insert_kernel(
    counts, offsets, classes, poses, spectra, defocus, probs, row_kernel, col_kernel,
    data_out, weight_out, row_pad, col_pad, weights, grids,
):
    slots, top = probs.shape
    pose_count, rows = row_kernel.shape[0], row_kernel.shape[1]
    grids[...] = jnp.zeros_like(grids)
    weights[...] = probs[...].astype(f32)
    band_row = lax.broadcasted_iota(jnp.int32, (BAND, IROWS), 0)
    band_col = lax.broadcasted_iota(jnp.int32, (BAND, IROWS), 1)
    pick_row = lax.broadcasted_iota(jnp.int32, (2 * ICOLS, ICOLS), 0)
    pick_col = lax.broadcasted_iota(jnp.int32, (2 * ICOLS, ICOLS), 1)
    pick_low = (pick_row == pick_col).astype(f32).astype(bf16)
    pick_high = (pick_row == pick_col + ICOLS).astype(f32).astype(bf16)

    def prepare(pose, carry):
        shift = (band_col == band_row + offsets[pose]).astype(f32).astype(bf16)
        placed = jnp.dot(row_kernel[pose], shift, preferred_element_type=f32)
        row_pad[pose] = placed.astype(bf16)
        dims = (((1,), (1,)), ((), ()))
        cols = col_kernel[pose]
        low = lax.dot_general(pick_low, cols, dims, preferred_element_type=f32)
        high = lax.dot_general(pick_high, cols, dims, preferred_element_type=f32)
        col_pad[pose, :, :LCOLS] = low.astype(bf16)
        col_pad[pose, :, LCOLS:] = high.astype(bf16)
        return carry

    lax.fori_loop(0, pose_count, prepare, 0, unroll=4)

    row_freq = lax.broadcasted_iota(jnp.int32, (IROWS, 2 * ICOLS), 0) - IROWS // 2
    col_freq = lax.broadcasted_iota(jnp.int32, (IROWS, 2 * ICOLS), 1) % ICOLS
    radius = (row_freq * row_freq + col_freq * col_freq).astype(f32) * (10.0 / (ICOLS * ICOLS))

    def insert(slot, carry):
        turns = defocus[pl.ds(slot, 1), :] * radius
        turns = turns - jnp.round(turns) + 0.1 / (2.0 * math.pi)
        ctf = sine_turns(turns)
        data = (ctf * spectra[slot].astype(f32)).astype(bf16)
        planes = jnp.concatenate([data, (ctf * ctf).astype(bf16)], axis=1)
        for k in range(top):
            pose = poses[slot, k]
            which = classes[slot, k]
            mixed = jnp.dot(row_pad[pose], planes, preferred_element_type=f32)
            mixed = (mixed * weights[pl.ds(slot, 1), k : k + 1]).astype(bf16)
            stacked = jnp.concatenate([mixed[:, : 2 * ICOLS], mixed[:, 2 * ICOLS :]], axis=0)
            spread = jnp.dot(stacked, col_pad[pose], preferred_element_type=f32)
            grids[which, :, : 2 * LCOLS] += spread[:rows]
            grids[which, :, 2 * LCOLS :] += spread[rows:, :LCOLS]
        return carry

    lax.fori_loop(0, counts[0], insert, 0)
    data_out[...] = grids[:, :, : 2 * LCOLS].astype(bf16)
    weight_out[...] = grids[:, :, 2 * LCOLS :].astype(bf16)


def dot3(a, b, dims=(((1,), (0,)), ((), ()))):
    mul = functools.partial(lax.dot_general, dimension_numbers=dims, preferred_element_type=f32)
    return mul(a[0], b[0]) + (mul(a[0], b[1]) + mul(a[1], b[0]))


def split(value):
    high = value.astype(bf16)
    return high, (value - high.astype(f32)).astype(bf16)


def reduce_kernel(
    sizes, data_part, weight_part, row_hbm, col_hbm, out_cols_hbm, out_rows_hbm, out,
    row_table, col_table, out_cols, out_rows,
    data_mate, data_sum, data_far, data_full, weight_mate, weight_sum, weight_far, weight_full,
    table_sem, mate_send, mate_recv, far_send, far_recv, full_send, full_recv,
    gather_send, gather_recv, pass_send, pass_recv,
):
    parts, sub, pair = sizes
    group = sub * pair
    chips = parts * pair // 2
    part, sub_at, pair_at = (lax.axis_index(axis) for axis in ("parts", "sub", "pair"))
    flat = part * pair + pair_at
    chip = flat // 2
    core = flat % 2
    member = sub_at * pair + pair_at

    def place(index):
        return {"parts": index // pair, "pair": index % pair}

    mate = place(2 * chip + 1 - core)

    def far(step):
        return lax.rem(chip + step, chips)

    def group_place(step):
        index = lax.rem(member + step, group)
        return {"sub": index // pair, "pair": index % pair}

    pieces = ((weight_part, weight_mate, weight_sum, weight_far, weight_full),
              (data_part, data_mate, data_sum, data_far, data_full))

    barrier = pltpu.get_barrier_semaphore()
    peers = [mate] + [place(2 * far(d) + core) for d in range(1, chips)]
    peers += [group_place(e) for e in range(1, group)]
    for peer in peers:
        pl.semaphore_signal(barrier, inc=1, device_id=peer, device_id_type=pl.DeviceIdType.MESH)
    loads = [
        pltpu.make_async_copy(source, target, table_sem.at[i])
        for i, (source, target) in enumerate((
            (row_hbm, row_table), (col_hbm, col_table),
            (out_cols_hbm.at[member], out_cols), (out_rows_hbm, out_rows),
        ))
    ]
    for load in loads:
        load.start()
    pl.semaphore_wait(barrier, len(peers))

    def remote(source, target, send, recv, device):
        return pltpu.make_async_remote_copy(
            src_ref=source, dst_ref=target, send_sem=send, recv_sem=recv,
            device_id=device, device_id_type=pl.DeviceIdType.MESH,
        )

    order = list(range(1, chips)) + [0]
    mate_copies = []
    for t, (local, from_mate, *_) in enumerate(pieces):
        for d in order:
            copy = remote(local.at[2 * far(d) + 1 - core], from_mate.at[d],
                          mate_send.at[t, d], mate_recv.at[t, d], mate)
            copy.start()
            mate_copies.append(copy)
    far_copies = [[], []]
    own = [None, None]
    for t, (local, from_mate, summed, from_far, _) in enumerate(pieces):
        for d in order:
            mate_copies[t * chips + order.index(d)].wait_recv()
            total = local[2 * far(d) + core].astype(f32) + from_mate[d].astype(f32)
            if d == 0:
                own[t] = total
                continue
            summed[d - 1] = total.astype(bf16)
            copy = remote(summed.at[d - 1], from_far.at[d - 1], far_send.at[t, d - 1],
                          far_recv.at[t, d - 1], place(2 * far(d) + core))
            copy.start()
            far_copies[t].append(copy)

    def finish(t):
        _, _, _, from_far, full = pieces[t]
        total = own[t]
        for d in range(1, chips):
            far_copies[t][d - 1].wait_recv()
            total = total + from_far[d - 1].astype(f32)
        full[member] = total.astype(bf16)
        copies = []
        for e in range(1, group):
            copy = remote(full.at[member], full.at[member], full_send.at[t, e - 1],
                          full_recv.at[t, e - 1], group_place(e))
            copy.start()
            copies.append(copy)
        return copies

    def arrive(t):
        full = pieces[t][4]
        for e in range(1, group):
            source = lax.rem(member + group - e, group)
            remote(full.at[source], full.at[source], full_send.at[t, e - 1],
                   full_recv.at[t, e - 1], group_place(e)).wait_recv()
        return full[...].reshape(LROWS, -1).astype(f32)

    group_copies = finish(0)
    loads[0].wait()
    loads[1].wait()
    weight = arrive(0)
    scale = jnp.ones_like(weight)
    rows_split = (row_table[0], row_table[1])
    cols_split = (col_table[0], col_table[1])
    for _ in range(ITERS):
        spread = dot3(split(weight * scale), cols_split)
        spread = jnp.concatenate([spread[:, :LCOLS], spread[:, LCOLS:]], axis=0)
        conv = dot3(rows_split, split(spread))
        scale = scale / jnp.maximum(jnp.abs(conv), floor_value)
    group_copies += finish(1)
    loads[2].wait()
    loads[3].wait()
    data = arrive(1) * jnp.concatenate([scale, scale], axis=1)
    turned = dot3((out_cols[0], out_cols[1]), split(data), (((1,), (1,)), ((), ())))
    block = turned.shape[0] // 2
    turned = jnp.concatenate([turned[:block], turned[block:]], axis=1)
    average = dot3(split(turned), (out_rows[0], out_rows[1]))
    out[part] = average.astype(bf16)

    last = []
    if pair == 1:
        def give(d):
            index = 2 * lax.rem(chip + chips - d, chips) + core
            copy = remote(out.at[index], out.at[index], pass_send.at[d], pass_recv.at[d], mate)
            copy.start()
            last.append(copy)
    for d in range(1, chips):
        copy = remote(out.at[part], out.at[part], gather_send.at[d - 1],
                      gather_recv.at[d - 1], place(2 * far(d) + core))
        copy.start()
        last.append(copy)
    if pair == 1:
        give(0)
    for d in range(1, chips):
        index = (2 * lax.rem(chip + chips - d, chips) + core) // pair
        remote(out.at[index], out.at[index], gather_send.at[d - 1], gather_recv.at[d - 1],
               place(2 * far(d) + core)).wait_recv()
        if pair == 1:
            give(d)
    if pair == 1:
        for d in range(chips):
            index = 2 * lax.rem(chip + chips - d, chips) + 1 - core
            remote(out.at[index], out.at[index], pass_send.at[d], pass_recv.at[d], mate).wait_recv()
    for copy in mate_copies + far_copies[0] + far_copies[1] + group_copies + last:
        copy.wait_send()


def per_device(spectra, defocus, classes, poses, probs, counts, offsets, row_kernel, col_kernel):
    parts, sub, pair = (lax.axis_size(axis) for axis in ("parts", "sub", "pair"))
    group = sub * pair
    count = parts * pair
    chips = count // 2
    rows = row_kernel.shape[1]
    own = rows // pair
    poses_n = row_kernel.shape[0]
    vmem = pl.BlockSpec(memory_space=pltpu.VMEM)
    smem = pl.BlockSpec(memory_space=pltpu.SMEM)
    anywhere = pl.BlockSpec(memory_space=pl.ANY)
    data, weight = pl.pallas_call(
        insert_kernel,
        out_shape=(
            jax.ShapeDtypeStruct((parts, rows, 2 * LCOLS), bf16),
            jax.ShapeDtypeStruct((parts, rows, LCOLS), bf16),
        ),
        in_specs=[smem] * 4 + [vmem] * 5,
        out_specs=(vmem, vmem),
        scratch_shapes=[
            pltpu.VMEM((poses_n, rows, IROWS), bf16),
            pltpu.VMEM((poses_n, 2 * ICOLS, 2 * LCOLS), bf16),
            pltpu.VMEM(probs.shape, f32),
            pltpu.VMEM((parts, rows, 3 * LCOLS), f32),
        ],
        compiler_params=pltpu.CompilerParams(vmem_limit_bytes=40 << 20),
    )(counts, offsets, classes, poses, spectra, defocus.astype(f32).reshape(-1, 1), probs,
      row_kernel, col_kernel)
    data = data.reshape(count, own, 2 * LCOLS)
    weight = weight.reshape(count, own, LCOLS)
    held = tables(group)
    scratch = [pltpu.VMEM(held[i].shape[1:] if i == 2 else held[i].shape, bf16) for i in range(4)]
    for width in (2 * LCOLS, LCOLS):
        scratch += [
            pltpu.VMEM((chips, own, width), bf16),
            pltpu.VMEM((chips - 1, own, width), bf16),
            pltpu.VMEM((chips - 1, own, width), bf16),
            pltpu.VMEM((group, own, width), bf16),
        ]
    scratch.append(pltpu.SemaphoreType.DMA((4,)))
    for shape in ((2, chips), (2, chips - 1), (2, group - 1), (chips - 1,), (chips,)):
        scratch += [pltpu.SemaphoreType.DMA(shape)] * 2
    averages = pl.pallas_call(
        functools.partial(reduce_kernel, (parts, sub, pair)),
        out_shape=jax.ShapeDtypeStruct((parts, BOX // group, BOX), bf16),
        in_specs=[vmem] * 2 + [anywhere] * 4,
        out_specs=vmem,
        scratch_shapes=scratch,
        compiler_params=pltpu.CompilerParams(
            collective_id=0, has_side_effects=True, vmem_limit_bytes=40 << 20
        ),
    )(data, weight, *[jnp.asarray(table) for table in held])
    return averages.astype(f32)


def solution(mesh):
    placed = (
        P(("groups", "parts", "pair"), None, None),
        P(("groups", "parts", "pair")),
        P(("groups", "parts", "pair"), None),
        P(("groups", "parts", "pair"), None),
        P(("groups", "parts", "pair"), None),
        P(("groups", "parts", "pair")),
        P(),
        P(None, "sub", None),
        P(),
    )
    return jax.shard_map(
        per_device,
        mesh=mesh,
        in_specs=placed,
        out_specs=P("groups", ("sub", "pair"), None),
        check_vma=False,
    )
```

profile of v0, /device:TPU:0, one launch (start us, length us, event | category | flops | bytes accessed | tf_op | source)
XLA Modules:
  0.0 47.6 jit_solution(399540748240326360)
XLA Ops:
  0.0 0.0 copy-start.10
  0.7 0.0 copy-done.10
  0.7 0.0 copy-start.9
  0.7 0.7 %copy-done.9 = bf16[16,4]{0,1:T(4,128)(2,1)S(1)} copy-done((bf16[16,4]{0,1:T(4,128)(2,1)S(1)}, bf16[16,4]{0,1:T(4,128)(2,1)}, u32[]{:S(2)}) %copy-start.9) | copy-done | bytes 152
  1.4 0.1 copy.17.probs
  1.5 0.0 copy-start.7
  1.5 0.1 copy.16.defocus
  1.5 0.6 %copy-done.7 = s32[16,4]{0,1:T(4,128)S(1)} copy-done((s32[16,4]{0,1:T(4,128)S(1)}, s32[16,4]{0,1:T(4,128)}, u32[]{:S(2)}) %copy-start.7) | copy-done | bytes 280
  2.1 0.0 copy-start.8
  2.1 0.1 copy.14.classes
  2.2 0.6 %copy-done.8 = s32[16,4]{0,1:T(4,128)S(1)} copy-done((s32[16,4]{0,1:T(4,128)S(1)}, s32[16,4]{0,1:T(4,128)}, u32[]{:S(2)}) %copy-start.8) | copy-done | bytes 280
  2.8 0.1 copy.15.poses
  2.9 0.0 copy-start.6
  2.9 1.6 %copy.18.row_kernel = bf16[32,128,64]{2,1,0:T(8,128)(2,1)S(1)} copy(bf16[32,128,64]{1,2,0:T(8,128)(2,1)} %param.20) | data formatting | bytes 1048576 | tf_op args[7]
  4.5 0.0 copy-done.6
  4.5 0.0 copy-start
  4.5 0.0 copy-start.5
  4.5 0.5 %copy.19.col_kernel = bf16[32,128,64]{2,1,0:T(8,128)(2,1)S(1)} copy(bf16[32,128,64]{1,2,0:T(8,128)(2,1)S(1)} %copy-done.6) | data formatting | bytes 1048576 | tf_op args[8]
  5.0 0.5 %copy-done = bf16[16,128,128]{2,1,0:T(8,128)(2,1)S(1)} copy-done((bf16[16,128,128]{2,1,0:T(8,128)(2,1)S(1)}, bf16[16,128,128]{2,1,0:T(8,128)(2,1)}, u32[]{:S(2)}) %copy-start) | copy-done | bytes 524312
  5.5 0.0 copy-done.5
  5.5 0.0 copy-start.1
  5.5 0.0 copy-start.2
  5.5 0.0 copy-start.3
  5.6 0.0 copy-start.4
  5.6 12.1 %shard_map.127 = (bf16[8,128,256]{2,1,0:T(8,128)(2,1)S(1)}, bf16[8,128,128]{2,1,0:T(8,128)(2,1)S(1)}) custom-call(s32[1]{0:T(128)S(6)} %copy.20.counts, s32[32]{0:T(128)S(1)} %copy-done.5, s32[16,4]{1,0:T(8,128)S(1)} %copy.14.classes, s32[16,4]{1,0:T(8,128)S(1)} %copy.15.poses, bf16[16,128,128]{2,1,0:T(8,128)(2,1)S(1)} %copy-done, ...), custom_call_target="tpu_custom_call" | custom-call | tf_op jit(solution)/shard_map/pallas_call | solution.py:304
  17.7 0.0 copy-done.1
  17.7 0.0 copy-done.2
  17.7 0.0 copy-done.3
  17.7 0.0 copy-done.4
  17.7 28.8 %shard_map.128 = bf16[8,128,256]{2,1,0:T(8,128)(2,1)S(1)} custom-call(bf16[8,128,256]{2,1,0:T(8,128)(2,1)S(1)} %get-tuple-element.7.data_part, bf16[8,128,128]{2,1,0:T(8,128)(2,1)S(1)} %get-tuple-element.8.weight_part, bf16[2,256,512]{2,1,0:T(8,128)(2,1)S(1)} %copy-done.3, bf16[2,128,256]{2,1,0:T(8,128)(2,1)S(1)} %copy-done.4, ...), custom_call_target="tpu_custom_call" | custom-call | tf_op jit(solution)/shard_map/pallas_call | solution.py:335
  46.6 1.1 %convert_element_type.4 = f32[8,128,256]{2,1,0:T(8,128)} convert(bf16[8,128,256]{2,1,0:T(8,128)(2,1)S(1)} %shard_map.128) | non-fusion elementwise | flops 262144 | bytes 1572864 | tf_op jit(solution)/shard_map/convert_element_type | solution.py:345
  (1 shorter events, 0.0 us)
Async XLA Ops:
  0.0 0.7 %copy-start.10 = (bf16[16]{0:T(256)(128)(2,1)S(1)}, bf16[16]{0:T(256)(128)(2,1)}, u32[]{:S(2)}) copy-start(bf16[16]{0:T(256)(128)(2,1)} %param.14) | copy-start | bytes 100
  0.7 0.7 %copy-start.9 = (bf16[16,4]{0,1:T(4,128)(2,1)S(1)}, bf16[16,4]{0,1:T(4,128)(2,1)}, u32[]{:S(2)}) copy-start(bf16[16,4]{0,1:T(4,128)(2,1)} %param.17) | copy-start | bytes 388
  1.5 0.7 %copy-start.7 = (s32[16,4]{0,1:T(4,128)S(1)}, s32[16,4]{0,1:T(4,128)}, u32[]{:S(2)}) copy-start(s32[16,4]{0,1:T(4,128)} %param.15) | copy-start | bytes 772
  2.1 0.7 %copy-start.8 = (s32[16,4]{0,1:T(4,128)S(1)}, s32[16,4]{0,1:T(4,128)}, u32[]{:S(2)}) copy-start(s32[16,4]{0,1:T(4,128)} %param.16) | copy-start | bytes 772
  2.9 1.6 %copy-start.6 = (bf16[32,128,64]{1,2,0:T(8,128)(2,1)S(1)}, bf16[32,128,64]{1,2,0:T(8,128)(2,1)}, u32[]{:S(2)}) copy-start(bf16[32,128,64]{1,2,0:T(8,128)(2,1)} %param.21) | copy-start | bytes 1572868
  4.5 1.0 %copy-start = (bf16[16,128,128]{2,1,0:T(8,128)(2,1)S(1)}, bf16[16,128,128]{2,1,0:T(8,128)(2,1)}, u32[]{:S(2)}) copy-start(bf16[16,128,128]{2,1,0:T(8,128)(2,1)} %spectra.1) | copy-start | bytes 1572868
  4.5 1.0 %copy-start.5 = (s32[32]{0:T(128)S(1)}, s32[32]{0:T(128)}, u32[]{:S(2)}) copy-start(s32[32]{0:T(128)} %offsets.1) | copy-start | bytes 388
  5.5 12.2 %copy-start.1 = (bf16[2,512,256]{2,1,0:T(8,128)(2,1)S(1)}, bf16[2,512,256]{2,1,0:T(8,128)(2,1)}, u32[]{:S(2)}) copy-start(bf16[2,512,256]{2,1,0:T(8,128)(2,1)} %constant.11.clone.out_rows_hbm) | copy-start | bytes 1572868
  5.5 12.2 %copy-start.2 = (bf16[2,2,256,256]{3,2,1,0:T(8,128)(2,1)S(1)}, bf16[2,2,256,256]{3,2,1,0:T(8,128)(2,1)}, u32[]{:S(2)}) copy-start(bf16[2,2,256,256]{3,2,1,0:T(8,128)(2,1)} %constant.10.clone.out_cols_hbm) | copy-start | bytes 1572868
  5.5 12.2 %copy-start.3 = (bf16[2,256,512]{2,1,0:T(8,128)(2,1)S(1)}, bf16[2,256,512]{2,1,0:T(8,128)(2,1)}, u32[]{:S(2)}) copy-start(bf16[2,256,512]{2,1,0:T(8,128)(2,1)} %constant.8.clone.row_hbm) | copy-start | bytes 1572868
  5.6 12.2 %copy-start.4 = (bf16[2,128,256]{2,1,0:T(8,128)(2,1)S(1)}, bf16[2,128,256]{2,1,0:T(8,128)(2,1)}, u32[]{:S(2)}) copy-start(bf16[2,128,256]{2,1,0:T(8,128)(2,1)} %constant.9.clone.col_hbm) | copy-start | bytes 393220
where the time goes:
time: 48.2 us; the launch traced here: 47.6 us
  Pallas kernels  40.9 us (85%)
  local copies, waits for them, and re-layouts  4.83 us (10%)
  other arithmetic  1.07 us (2%)
  between operations  0.79 us (2%)
    pallas_call x1, Pallas kernels, per_device(): pl.pallas_call(functools.partial(reduce_kernel, (parts, sub, pair)), out_...  28.8 us
    pallas_call x1, Pallas kernels, per_device(): pl.pallas_call(insert_kernel, out_shape=(jax.ShapeDtypeStruct((parts, row...  12.1 us
    unnamed x27, local copies, waits for them, and re-layouts  4.74 us
    convert_element_type x1, other arithmetic, per_device(): return averages.astype(f32)  1.06 us

commit v1 on v0

--- a/solution.py
+++ b/solution.py
@@ -77,56 +77,56 @@
 
 
 def insert_kernel(
-    counts, offsets, classes, poses, spectra, defocus, probs, row_kernel, col_kernel,
-    data_out, weight_out, row_pad, col_pad, weights, grids,
+    counts, offsets, classes, poses, defocus, probs, spectra, row_kernel, col_kernel,
+    data_out, weight_out, row_pad, col_pad, grids,
 ):
-    slots, top = probs.shape
-    pose_count, rows = row_kernel.shape[0], row_kernel.shape[1]
+    top, slots = probs.shape
+    pose_count, rows = row_kernel.shape[0], row_kernel.shape[2]
     grids[...] = jnp.zeros_like(grids)
-    weights[...] = probs[...].astype(f32)
+    col_pad[...] = jnp.zeros_like(col_pad)
     band_row = lax.broadcasted_iota(jnp.int32, (BAND, IROWS), 0)
     band_col = lax.broadcasted_iota(jnp.int32, (BAND, IROWS), 1)
-    pick_row = lax.broadcasted_iota(jnp.int32, (2 * ICOLS, ICOLS), 0)
-    pick_col = lax.broadcasted_iota(jnp.int32, (2 * ICOLS, ICOLS), 1)
-    pick_low = (pick_row == pick_col).astype(f32).astype(bf16)
-    pick_high = (pick_row == pick_col + ICOLS).astype(f32).astype(bf16)
+    band_gap = band_col - band_row
 
     def prepare(pose, carry):
-        shift = (band_col == band_row + offsets[pose]).astype(f32).astype(bf16)
-        placed = jnp.dot(row_kernel[pose], shift, preferred_element_type=f32)
+        shift = (band_gap == offsets[pose]).astype(f32).astype(bf16)
+        placed = lax.dot_general(
+            row_kernel[pose], shift, (((0,), (0,)), ((), ())), preferred_element_type=f32
+        )
         row_pad[pose] = placed.astype(bf16)
-        dims = (((1,), (1,)), ((), ()))
-        cols = col_kernel[pose]
-        low = lax.dot_general(pick_low, cols, dims, preferred_element_type=f32)
-        high = lax.dot_general(pick_high, cols, dims, preferred_element_type=f32)
-        col_pad[pose, :, :LCOLS] = low.astype(bf16)
-        col_pad[pose, :, LCOLS:] = high.astype(bf16)
+        col_pad[pose, :ICOLS, :LCOLS] = col_kernel[pose]
+        col_pad[pose, ICOLS:, LCOLS:] = col_kernel[pose]
         return carry
 
-    lax.fori_loop(0, pose_count, prepare, 0, unroll=4)
+    lax.fori_loop(0, pose_count, prepare, 0, unroll=8)
 
     row_freq = lax.broadcasted_iota(jnp.int32, (IROWS, 2 * ICOLS), 0) - IROWS // 2
     col_freq = lax.broadcasted_iota(jnp.int32, (IROWS, 2 * ICOLS), 1) % ICOLS
     radius = (row_freq * row_freq + col_freq * col_freq).astype(f32) * (10.0 / (ICOLS * ICOLS))
 
     def insert(slot, carry):
-        turns = defocus[pl.ds(slot, 1), :] * radius
+        used = slot < counts[0]
+        turns = defocus[slot] * radius
         turns = turns - jnp.round(turns) + 0.1 / (2.0 * math.pi)
         ctf = sine_turns(turns)
         data = (ctf * spectra[slot].astype(f32)).astype(bf16)
         planes = jnp.concatenate([data, (ctf * ctf).astype(bf16)], axis=1)
-        for k in range(top):
-            pose = poses[slot, k]
-            which = classes[slot, k]
-            mixed = jnp.dot(row_pad[pose], planes, preferred_element_type=f32)
-            mixed = (mixed * weights[pl.ds(slot, 1), k : k + 1]).astype(bf16)
+        pose_set = [poses[k, slot] for k in range(top)]
+        row_set = jnp.concatenate([row_pad[pose] for pose in pose_set], axis=0)
+        mixed_set = jnp.dot(row_set, planes, preferred_element_type=f32)
+        spread_set = []
+        for k, pose in enumerate(pose_set):
+            weight = jnp.where(used, probs[k, slot], 0.0)
+            mixed = (mixed_set[k * rows : (k + 1) * rows] * weight).astype(bf16)
             stacked = jnp.concatenate([mixed[:, : 2 * ICOLS], mixed[:, 2 * ICOLS :]], axis=0)
-            spread = jnp.dot(stacked, col_pad[pose], preferred_element_type=f32)
+            spread_set.append(jnp.dot(stacked, col_pad[pose], preferred_element_type=f32))
+        for k, spread in enumerate(spread_set):
+            which = classes[k, slot]
             grids[which, :, : 2 * LCOLS] += spread[:rows]
             grids[which, :, 2 * LCOLS :] += spread[rows:, :LCOLS]
         return carry
 
-    lax.fori_loop(0, counts[0], insert, 0)
+    lax.fori_loop(0, slots, insert, 0, unroll=2)
     data_out[...] = grids[:, :, : 2 * LCOLS].astype(bf16)
     weight_out[...] = grids[:, :, 2 * LCOLS :].astype(bf16)
 
@@ -307,17 +307,16 @@
             jax.ShapeDtypeStruct((parts, rows, 2 * LCOLS), bf16),
             jax.ShapeDtypeStruct((parts, rows, LCOLS), bf16),
         ),
-        in_specs=[smem] * 4 + [vmem] * 5,
+        in_specs=[smem] * 6 + [vmem] * 3,
         out_specs=(vmem, vmem),
         scratch_shapes=[
             pltpu.VMEM((poses_n, rows, IROWS), bf16),
             pltpu.VMEM((poses_n, 2 * ICOLS, 2 * LCOLS), bf16),
-            pltpu.VMEM(probs.shape, f32),
             pltpu.VMEM((parts, rows, 3 * LCOLS), f32),
         ],
         compiler_params=pltpu.CompilerParams(vmem_limit_bytes=40 << 20),
-    )(counts, offsets, classes, poses, spectra, defocus.astype(f32).reshape(-1, 1), probs,
-      row_kernel, col_kernel)
+    )(counts, offsets, classes.T, poses.T, defocus.astype(f32), probs.T.astype(f32), spectra,
+      jnp.swapaxes(row_kernel, 1, 2), jnp.swapaxes(col_kernel, 1, 2))
     data = data.reshape(count, own, 2 * LCOLS)
     weight = weight.reshape(count, own, LCOLS)
     held = tables(group)

time: 48.2 us -> 43.3 us (0.90)
  Pallas kernels: 40.9 us -> 35.3 us
  local copies, waits for them, and re-layouts: 4.83 us -> 5.37 us
    pallas_call x1, Pallas kernels: 12.1 us -> 8.37 us  [per_device(): pl.pallas_call(insert_kernel, out_shape=(jax.ShapeDtypeStruct((parts, row...]
    pallas_call x1, Pallas kernels: 28.8 us -> 27 us  [per_device(): pl.pallas_call(functools.partial(reduce_kernel, (parts, sub, pair)), out_...]
    unnamed x27 -> x24, local copies, waits for them, and re-layouts: 4.74 us -> 5.37 us
where the time goes in v1:
time: 43.3 us; the launch traced here: 42.5 us
  Pallas kernels  35.3 us (82%)
  local copies, waits for them, and re-layouts  5.37 us (12%)
  other arithmetic  1.07 us (2%)
  between operations  0.73 us (2%)
    pallas_call x1, Pallas kernels, per_device(): pl.pallas_call(functools.partial(reduce_kernel, (parts, sub, pair)), out_...  27 us
    pallas_call x1, Pallas kernels, per_device(): pl.pallas_call(insert_kernel, out_shape=(jax.ShapeDtypeStruct((parts, row...  8.37 us
    unnamed x24, local copies, waits for them, and re-layouts  5.37 us
    convert_element_type x1, other arithmetic, per_device(): return averages.astype(f32)  1.06 us

profile of v1, /device:TPU:0, one launch (start us, length us, event | category | flops | bytes accessed | tf_op | source)
XLA Modules:
  0.0 42.5 jit_solution(10441469224664155457)
XLA Ops:
  0.7 0.0 copy-start.11
  0.7 0.0 copy-start.10
  0.7 0.6 %copy-done.11 = bf16[16]{0:T(256)(128)(2,1)S(1)} copy-done((bf16[16]{0:T(256)(128)(2,1)S(1)}, bf16[16]{0:T(256)(128)(2,1)}, u32[]{:S(2)}) %copy-start.11) | copy-done | bytes 56
  1.3 0.0 copy-start.7
  1.3 0.0 copy-start.8
  1.3 0.0 copy-done.10
  1.3 0.0 copy-start.9
  1.4 0.6 %copy-done.7 = s32[16,4]{0,1:T(4,128)S(1)} copy-done((s32[16,4]{0,1:T(4,128)S(1)}, s32[16,4]{0,1:T(4,128)}, u32[]{:S(2)}) %copy-start.7) | copy-done | bytes 280
  2.0 0.0 copy-done.8
  2.0 0.0 copy-done.9
  2.0 0.0 copy-start
  2.0 1.0 %copy-done = bf16[16,128,128]{2,1,0:T(8,128)(2,1)S(1)} copy-done((bf16[16,128,128]{2,1,0:T(8,128)(2,1)S(1)}, bf16[16,128,128]{2,1,0:T(8,128)(2,1)}, u32[]{:S(2)}) %copy-start) | copy-done | bytes 524312
  3.1 0.0 copy-start.1
  3.1 1.0 %copy-done.1 = bf16[32,128,64]{1,2,0:T(8,128)(2,1)S(1)} copy-done((bf16[32,128,64]{1,2,0:T(8,128)(2,1)S(1)}, bf16[32,128,64]{1,2,0:T(8,128)(2,1)}, u32[]{:S(2)}) %copy-start.1) | copy-done | bytes 524312
  4.1 0.0 copy-start.2
  4.1 1.0 %copy-done.2 = bf16[32,128,64]{1,2,0:T(8,128)(2,1)S(1)} copy-done((bf16[32,128,64]{1,2,0:T(8,128)(2,1)S(1)}, bf16[32,128,64]{1,2,0:T(8,128)(2,1)}, u32[]{:S(2)}) %copy-start.2) | copy-done | bytes 524312
  5.1 0.0 copy-start.3
  5.1 0.0 copy-start.4
  5.1 0.0 copy-start.5
  5.1 8.4 %shard_map.127 = (bf16[8,128,256]{2,1,0:T(8,128)(2,1)S(1)}, bf16[8,128,128]{2,1,0:T(8,128)(2,1)S(1)}) custom-call(s32[1]{0:T(128)S(6)} %copy.14.counts, s32[32]{0:T(128)S(1)} %copy-done.9, s32[4,16]{1,0:T(4,128)S(1)} %bitcast.8, s32[4,16]{1,0:T(4,128)S(1)} %bitcast.9, f32[16]{0:T(128)S(1)} %convert_element_type.11.defocus, ...), custom_call_target="tpu_custom_call" | custom-call | tf_op jit(solution)/shard_map/pallas_call | solution.py:304
  13.5 0.0 copy-done.3
  13.5 0.0 copy-done.4
  13.5 0.0 copy-done.5
  13.5 0.0 copy-start.6
  13.6 0.9 %copy-done.6 = bf16[2,128,256]{2,1,0:T(8,128)(2,1)S(1)} copy-done((bf16[2,128,256]{2,1,0:T(8,128)(2,1)S(1)}, bf16[2,128,256]{2,1,0:T(8,128)(2,1)}, u32[]{:S(2)}) %copy-start.6) | copy-done | bytes 131096
  14.5 27.0 %shard_map.128 = bf16[8,128,256]{2,1,0:T(8,128)(2,1)S(1)} custom-call(bf16[8,128,256]{2,1,0:T(8,128)(2,1)S(1)} %get-tuple-element.7.data_part, bf16[8,128,128]{2,1,0:T(8,128)(2,1)S(1)} %get-tuple-element.8.weight_part, bf16[2,256,512]{2,1,0:T(8,128)(2,1)S(1)} %copy-done.5, bf16[2,128,256]{2,1,0:T(8,128)(2,1)S(1)} %copy-done.6, ...), custom_call_target="tpu_custom_call" | custom-call | tf_op jit(solution)/shard_map/pallas_call | solution.py:334
  41.4 1.1 %convert_element_type.14 = f32[8,128,256]{2,1,0:T(8,128)} convert(bf16[8,128,256]{2,1,0:T(8,128)(2,1)S(1)} %shard_map.128) | non-fusion elementwise | flops 262144 | bytes 1572864 | tf_op jit(solution)/shard_map/convert_element_type | solution.py:344
  (2 shorter events, 0.0 us)
Async XLA Ops:
  0.7 0.7 %copy-start.11 = (bf16[16]{0:T(256)(128)(2,1)S(1)}, bf16[16]{0:T(256)(128)(2,1)}, u32[]{:S(2)}) copy-start(bf16[16]{0:T(256)(128)(2,1)} %param.14) | copy-start | bytes 100
  0.7 0.7 %copy-start.10 = (bf16[16,4]{0,1:T(4,128)(2,1)S(1)}, bf16[16,4]{0,1:T(4,128)(2,1)}, u32[]{:S(2)}) copy-start(bf16[16,4]{0,1:T(4,128)(2,1)} %param.17) | copy-start | bytes 388
  1.3 0.7 %copy-start.7 = (s32[16,4]{0,1:T(4,128)S(1)}, s32[16,4]{0,1:T(4,128)}, u32[]{:S(2)}) copy-start(s32[16,4]{0,1:T(4,128)} %param.15) | copy-start | bytes 772
  1.3 0.7 %copy-start.8 = (s32[16,4]{0,1:T(4,128)S(1)}, s32[16,4]{0,1:T(4,128)}, u32[]{:S(2)}) copy-start(s32[16,4]{0,1:T(4,128)} %param.16) | copy-start | bytes 772
  1.3 0.7 %copy-start.9 = (s32[32]{0:T(128)S(1)}, s32[32]{0:T(128)}, u32[]{:S(2)}) copy-start(s32[32]{0:T(128)} %offsets.1) | copy-start | bytes 388
  2.0 1.0 %copy-start = (bf16[16,128,128]{2,1,0:T(8,128)(2,1)S(1)}, bf16[16,128,128]{2,1,0:T(8,128)(2,1)}, u32[]{:S(2)}) copy-start(bf16[16,128,128]{2,1,0:T(8,128)(2,1)} %spectra.1) | copy-start | bytes 1572868
  3.1 1.0 %copy-start.1 = (bf16[32,128,64]{1,2,0:T(8,128)(2,1)S(1)}, bf16[32,128,64]{1,2,0:T(8,128)(2,1)}, u32[]{:S(2)}) copy-start(bf16[32,128,64]{1,2,0:T(8,128)(2,1)} %param.20) | copy-start | bytes 1572868
  4.1 1.0 %copy-start.2 = (bf16[32,128,64]{1,2,0:T(8,128)(2,1)S(1)}, bf16[32,128,64]{1,2,0:T(8,128)(2,1)}, u32[]{:S(2)}) copy-start(bf16[32,128,64]{1,2,0:T(8,128)(2,1)} %param.21) | copy-start | bytes 1572868
  5.1 8.4 %copy-start.3 = (bf16[2,512,256]{2,1,0:T(8,128)(2,1)S(1)}, bf16[2,512,256]{2,1,0:T(8,128)(2,1)}, u32[]{:S(2)}) copy-start(bf16[2,512,256]{2,1,0:T(8,128)(2,1)} %constant.11.clone.out_rows_hbm) | copy-start | bytes 1572868
  5.1 8.4 %copy-start.4 = (bf16[2,2,256,256]{3,2,1,0:T(8,128)(2,1)S(1)}, bf16[2,2,256,256]{3,2,1,0:T(8,128)(2,1)}, u32[]{:S(2)}) copy-start(bf16[2,2,256,256]{3,2,1,0:T(8,128)(2,1)} %constant.10.clone.out_cols_hbm) | copy-start | bytes 1572868
  5.1 8.4 %copy-start.5 = (bf16[2,256,512]{2,1,0:T(8,128)(2,1)S(1)}, bf16[2,256,512]{2,1,0:T(8,128)(2,1)}, u32[]{:S(2)}) copy-start(bf16[2,256,512]{2,1,0:T(8,128)(2,1)} %constant.8.clone.row_hbm) | copy-start | bytes 1572868
  13.5 0.9 %copy-start.6 = (bf16[2,128,256]{2,1,0:T(8,128)(2,1)S(1)}, bf16[2,128,256]{2,1,0:T(8,128)(2,1)}, u32[]{:S(2)}) copy-start(bf16[2,128,256]{2,1,0:T(8,128)(2,1)} %constant.9.clone.col_hbm) | copy-start | bytes 393220

commit v2 on v1

--- a/solution.py
+++ b/solution.py
@@ -24,6 +24,9 @@
 
 f32 = jnp.float32
 bf16 = jnp.bfloat16
+
+vmem_whole = 67043328
+spare = 500 << 10
 
 
 def split_np(table):
@@ -77,16 +80,27 @@
 
 
 def insert_kernel(
-    counts, offsets, classes, poses, defocus, probs, spectra, row_kernel, col_kernel,
-    data_out, weight_out, row_pad, col_pad, grids,
+    counts, offsets, classes, poses, defocus, probs, spectra_hbm, row_hbm, col_hbm,
+    data_out, weight_out, row_pad, col_pad, grids, spectra, row_kernel, col_kernel, load_sem,
 ):
     top, slots = probs.shape
     pose_count, rows = row_kernel.shape[0], row_kernel.shape[2]
+    loads = [
+        pltpu.make_async_copy(source, target, load_sem.at[i])
+        for i, (source, target) in enumerate((
+            (row_hbm, row_kernel), (col_hbm, col_kernel), (spectra_hbm, spectra),
+        ))
+    ]
+    for load in loads:
+        load.start()
     grids[...] = jnp.zeros_like(grids)
     col_pad[...] = jnp.zeros_like(col_pad)
     band_row = lax.broadcasted_iota(jnp.int32, (BAND, IROWS), 0)
     band_col = lax.broadcasted_iota(jnp.int32, (BAND, IROWS), 1)
     band_gap = band_col - band_row
+
+    loads[0].wait()
+    loads[1].wait()
 
     def prepare(pose, carry):
         shift = (band_gap == offsets[pose]).astype(f32).astype(bf16)
@@ -100,6 +114,7 @@
 
     lax.fori_loop(0, pose_count, prepare, 0, unroll=8)
 
+    loads[2].wait()
     row_freq = lax.broadcasted_iota(jnp.int32, (IROWS, 2 * ICOLS), 0) - IROWS // 2
     col_freq = lax.broadcasted_iota(jnp.int32, (IROWS, 2 * ICOLS), 1) % ICOLS
     radius = (row_freq * row_freq + col_freq * col_freq).astype(f32) * (10.0 / (ICOLS * ICOLS))
@@ -298,23 +313,29 @@
     rows = row_kernel.shape[1]
     own = rows // pair
     poses_n = row_kernel.shape[0]
+    partial = 2 * parts * rows * 3 * LCOLS
+    result = 2 * parts * (BOX // group) * BOX
     vmem = pl.BlockSpec(memory_space=pltpu.VMEM)
     smem = pl.BlockSpec(memory_space=pltpu.SMEM)
-    anywhere = pl.BlockSpec(memory_space=pl.ANY)
+    hbm = pl.BlockSpec(memory_space=pltpu.HBM)
     data, weight = pl.pallas_call(
         insert_kernel,
         out_shape=(
             jax.ShapeDtypeStruct((parts, rows, 2 * LCOLS), bf16),
             jax.ShapeDtypeStruct((parts, rows, LCOLS), bf16),
         ),
-        in_specs=[smem] * 6 + [vmem] * 3,
+        in_specs=[smem] * 6 + [hbm] * 3,
         out_specs=(vmem, vmem),
         scratch_shapes=[
             pltpu.VMEM((poses_n, rows, IROWS), bf16),
             pltpu.VMEM((poses_n, 2 * ICOLS, 2 * LCOLS), bf16),
             pltpu.VMEM((parts, rows, 3 * LCOLS), f32),
+            pltpu.VMEM(spectra.shape, bf16),
+            pltpu.VMEM((poses_n, BAND, rows), bf16),
+            pltpu.VMEM((poses_n, ICOLS, LCOLS), bf16),
+            pltpu.SemaphoreType.DMA((3,)),
         ],
-        compiler_params=pltpu.CompilerParams(vmem_limit_bytes=40 << 20),
+        compiler_params=pltpu.CompilerParams(vmem_limit_bytes=vmem_whole - partial - spare),
     )(counts, offsets, classes.T, poses.T, defocus.astype(f32), probs.T.astype(f32), spectra,
       jnp.swapaxes(row_kernel, 1, 2), jnp.swapaxes(col_kernel, 1, 2))
     data = data.reshape(count, own, 2 * LCOLS)
@@ -334,11 +355,11 @@
     averages = pl.pallas_call(
         functools.partial(reduce_kernel, (parts, sub, pair)),
         out_shape=jax.ShapeDtypeStruct((parts, BOX // group, BOX), bf16),
-        in_specs=[vmem] * 2 + [anywhere] * 4,
+        in_specs=[vmem] * 2 + [hbm] * 4,
         out_specs=vmem,
         scratch_shapes=scratch,
         compiler_params=pltpu.CompilerParams(
-            collective_id=0, has_side_effects=True, vmem_limit_bytes=40 << 20
+            collective_id=0, has_side_effects=True, vmem_limit_bytes=vmem_whole - partial - result - spare
         ),
     )(data, weight, *[jnp.asarray(table) for table in held])
     return averages.astype(f32)

time: 43.3 us -> 44.6 us (1.030)
  local copies, waits for them, and re-layouts: 5.37 us -> 0.79 us
  Pallas kernels: 35.3 us -> 39.2 us
  other arithmetic: 1.07 us -> 3.22 us
    unnamed x24 -> x4, local copies, waits for them, and re-layouts: 5.37 us -> 0.79 us
    pallas_call x1, Pallas kernels: 8.37 us -> 10.3 us  [per_device(): pl.pallas_call(insert_kernel, out_shape=(jax.ShapeDtypeStruct((parts, row...]
    pallas_call x1, Pallas kernels: 27 us -> 28.9 us  [per_device(): pl.pallas_call(functools.partial(reduce_kernel, (parts, sub, pair)), out_...]
    convert_element_type x1, other arithmetic: 1.06 us -> 2.11 us  [per_device(): return averages.astype(f32)]
    convert_element_type x1, other arithmetic: 0.01 us -> 0.58 us  [per_device(): probs.T.astype(f32)]
    convert_element_type x1, other arithmetic: 0.01 us -> 0.54 us  [per_device(): defocus.astype(f32)]
where the time goes in v2:
time: 44.6 us; the launch traced here: 43.9 us
  Pallas kernels  39.2 us (88%)
  other arithmetic  3.22 us (7%)
  local copies, waits for them, and re-layouts  0.79 us (2%)
  between operations  0.68 us (2%)
    pallas_call x1, Pallas kernels, per_device(): pl.pallas_call(functools.partial(reduce_kernel, (parts, sub, pair)), out_...  28.9 us
    pallas_call x1, Pallas kernels, per_device(): pl.pallas_call(insert_kernel, out_shape=(jax.ShapeDtypeStruct((parts, row...  10.3 us
    convert_element_type x1, other arithmetic, per_device(): return averages.astype(f32)  2.11 us

profile of v2, /device:TPU:0, one launch (start us, length us, event | category | flops | bytes accessed | tf_op | source)
XLA Modules:
  0.0 43.9 jit_solution(2468637419061286948)
XLA Ops:
  0.7 0.0 copy-start.1
  0.7 0.6 %copy-done.1 = bf16[16]{0:T(256)(128)(2,1)S(1)} copy-done((bf16[16]{0:T(256)(128)(2,1)S(1)}, bf16[16]{0:T(256)(128)(2,1)}, u32[]{:S(2)}) %copy-start.1) | copy-done | bytes 56
  1.3 0.0 copy-start
  1.3 0.5 %convert_element_type.11.defocus = f32[16]{0:T(128)} convert(bf16[16]{0:T(256)(128)(2,1)S(1)} %copy-done.1) | non-fusion elementwise | flops 16 | bytes 96 | tf_op jit(solution)/shard_map/convert_element_type | solution.py:339
  1.9 0.1 copy-done
  2.0 0.6 %convert_bitcast_fusion.probs = f32[4,16]{1,0:T(4,128)} fusion(bf16[16,4]{0,1:T(4,128)(2,1)S(1)} %copy-done), kind=kLoop, calls=%fused_computation | loop fusion | flops 64 | bytes 384 | tf_op jit(solution)/shard_map/convert_element_type | solution.py:339
  2.6 10.3 %shard_map.127 = (bf16[8,128,256]{2,1,0:T(8,128)(2,1)}, bf16[8,128,128]{2,1,0:T(8,128)(2,1)}) custom-call(s32[1]{0:T(128)S(6)} %copy.14.counts, s32[32]{0:T(128)} %offsets.1, s32[4,16]{1,0:T(4,128)} %bitcast.8, s32[4,16]{1,0:T(4,128)} %bitcast.9, f32[16]{0:T(128)} %convert_element_type.11.defocus, f32[4,16]{1,0:T(4,128)} %convert_bitcast_fusion.probs, ...), custom_call_target="tpu_custom_call" | custom-call | tf_op jit(solution)/shard_map/pallas_call | solution.py:321
  12.9 28.9 %shard_map.128 = bf16[8,128,256]{2,1,0:T(8,128)(2,1)} custom-call(bf16[8,128,256]{2,1,0:T(8,128)(2,1)} %get-tuple-element.7.data_part, bf16[8,128,128]{2,1,0:T(8,128)(2,1)} %get-tuple-element.8.weight_part, bf16[2,256,512]{2,1,0:T(8,128)(2,1)} %constant.8.clone.row_hbm, bf16[2,128,256]{2,1,0:T(8,128)(2,1)} %constant.9.clone.col_hbm, ...), custom_call_target="tpu_custom_call" | custom-call | tf_op jit(solution)/shard_map/pallas_call | solution.py:355
  41.8 2.1 %convert_element_type.14 = f32[8,128,256]{2,1,0:T(8,128)} convert(bf16[8,128,256]{2,1,0:T(8,128)(2,1)} %shard_map.128) | non-fusion elementwise | flops 262144 | bytes 1572864 | tf_op jit(solution)/shard_map/convert_element_type | solution.py:365
Async XLA Ops:
  0.7 0.7 %copy-start.1 = (bf16[16]{0:T(256)(128)(2,1)S(1)}, bf16[16]{0:T(256)(128)(2,1)}, u32[]{:S(2)}) copy-start(bf16[16]{0:T(256)(128)(2,1)} %param.14) | copy-start | bytes 100
  1.3 0.7 %copy-start = (bf16[16,4]{0,1:T(4,128)(2,1)S(1)}, bf16[16,4]{0,1:T(4,128)(2,1)}, u32[]{:S(2)}) copy-start(bf16[16,4]{0,1:T(4,128)(2,1)} %param.17) | copy-start | bytes 388
